TPU v7x, 32 devices: a whole 2x2x4 slice. The times are simulated.
32 devices in a mesh: kt: 8 (over z, y), tile: 4 (over x, core).
Axes of the slice: x: 2, y: 2, z: 4, core: 2. Of those that a mesh axis runs over, the one named last changes fastest.
Arguments:
- green_particle: bfloat16 [2, 64, 1024, 1024], P(None, 'kt', 'tile'), may hold values from -6 to 6
- green_hole: bfloat16 [2, 64, 1024, 1024], P(None, 'kt', 'tile'), may hold values from -6 to 6
- coulomb: bfloat16 [2, 64, 1024, 1024], P(None, 'kt'), may hold values from -3 to 3
Outputs:
- screened: float32 [2, 64, 1024, 1024], P(None, 'kt', 'tile')
All inputs are finite; a program needn't handle non-finite values.
Results may differ from a plain program's by a relative error of at most 0.0039.
Values may be sent and summed in bfloat16 or wider, within the bound.
No kernel may reach another device: no remote copies, remote signals or barrier semaphores. Data moves between devices by JAX's collectives and lax.ppermute only.
A program may use at most 192 MiB of HBM per device.

v0:
```python
import math
import jax
import jax.numpy as jnp
from jax import lax
from jax.sharding import PartitionSpec as P

KSIDE = 4
K = 64
HIGHEST = lax.Precision.HIGHEST


def phase_tables(points, side_count):
    point_index = jnp.arange(points, dtype=jnp.int32)
    digit_high = point_index // (side_count * side_count)
    digit_mid = point_index // side_count % side_count
    digit_low = point_index % side_count
    phase_turns = (
        digit_high[:, None] * digit_high[None, :]
        + digit_mid[:, None] * digit_mid[None, :]
        + digit_low[:, None] * digit_low[None, :]
    ) % side_count
    angles = phase_turns.astype(jnp.float32) * (2.0 * math.pi / side_count)
    return (jnp.cos(angles) / points, jnp.sin(angles) / points)


def to_cells(real_part, imag_part, cosine_table, sine_table):
    return (
        jnp.dot(cosine_table, real_part, precision=HIGHEST)
        - jnp.dot(sine_table, imag_part, precision=HIGHEST),
        jnp.dot(sine_table, real_part, precision=HIGHEST)
        + jnp.dot(cosine_table, imag_part, precision=HIGHEST),
    )


def to_momenta(real_part, imag_part, cosine_table, sine_table):
    return (
        jnp.dot(cosine_table, real_part, precision=HIGHEST)
        + jnp.dot(sine_table, imag_part, precision=HIGHEST),
        jnp.dot(cosine_table, imag_part, precision=HIGHEST)
        - jnp.dot(sine_table, real_part, precision=HIGHEST),
    )


def polarize(particle, hole_part):
    cosine_table, sine_table = phase_tables(K, KSIDE)
    part_real, part_imag = to_cells(
        particle[0].astype(jnp.float32), particle[1].astype(jnp.float32), cosine_table, sine_table
    )
    hole_real, hole_imag = to_cells(
        hole_part[0].astype(jnp.float32), hole_part[1].astype(jnp.float32), cosine_table, sine_table
    )
    cell_real = part_real * hole_real - part_imag * hole_imag
    cell_imag = part_real * hole_imag + part_imag * hole_real
    mom_real, mom_imag = to_momenta(cell_real, cell_imag, cosine_table, sine_table)
    return jnp.stack([mom_real, mom_imag]).astype(jnp.bfloat16)


def product_of(left_side, right_side):
    return jnp.einsum("kij,kjl->kil", left_side, right_side, preferred_element_type=jnp.float32)


def complex_batched(left_real, left_imag, right_real, right_imag):
    real_out = product_of(left_real, right_real) - product_of(left_imag, right_imag)
    imag_out = product_of(left_real, right_imag) + product_of(left_imag, right_real)
    return (real_out, imag_out)


def body(green_particle, green_hole, coulomb):
    tile_rows = green_particle.shape[2]
    moved_part, moved_hole = (
        lax.all_to_all(green_particle, "kt", split_axis=3, concat_axis=1, tiled=True),
        lax.all_to_all(green_hole, "kt", split_axis=3, concat_axis=1, tiled=True),
    )
    points = moved_part.shape[1]
    narrow = moved_part.shape[3]
    polar_q = polarize(
        moved_part.reshape(2, points, tile_rows * narrow),
        moved_hole.reshape(2, points, tile_rows * narrow),
    )
    polar_q = polar_q.reshape(2, points, tile_rows, narrow)
    polar_rows = lax.all_to_all(polar_q, "kt", split_axis=1, concat_axis=3, tiled=True)
    mid_real, mid_imag = complex_batched(polar_rows[0], polar_rows[1], coulomb[0], coulomb[1])
    mid_stack = jnp.stack([mid_real.astype(jnp.bfloat16), mid_imag.astype(jnp.bfloat16)])
    row_start = lax.axis_index("tile") * tile_rows
    coulomb_rows = lax.dynamic_slice_in_dim(coulomb, row_start, tile_rows, 2)
    segment = lax.all_gather(mid_stack, "tile", axis=2, tiled=True)
    left_real = coulomb_rows[0]
    left_imag = coulomb_rows[1]
    more_real, more_imag = complex_batched(left_real, left_imag, segment[0], segment[1])
    summed = jnp.stack([more_real, more_imag])
    return coulomb_rows.astype(jnp.float32) + summed


def solution(mesh):
    return jax.shard_map(
        body,
        mesh=mesh,
        in_specs=(
            P(None, "kt", "tile", None),
            P(None, "kt", "tile", None),
            P(None, "kt", None, None),
        ),
        out_specs=P(None, "kt", "tile", None),
        check_vma=False,
    )
```

profile of v0, /device:TPU:0, one launch (start us, length us, event | category | flops | bytes accessed | tf_op | source)
XLA Modules:
  0.0 1116.9 jit_solution(6014429570869471573)
XLA Ops:
  6.5 12.6 %copy.8 = bf16[2,8,256,1024]{2,1,0,3:T(8,128)(2,1)} copy(bf16[2,8,256,1024]{3,2,1,0:T(8,128)(2,1)} %param.3) | data formatting | bytes 16777216 | tf_op args[0]
  19.1 7.3 all-to-all-start
  26.4 12.5 %copy.10 = bf16[2,8,256,1024]{2,1,0,3:T(8,128)(2,1)} copy(bf16[2,8,256,1024]{3,2,1,0:T(8,128)(2,1)} %param.4) | data formatting | bytes 16777216 | tf_op args[1]
  38.9 170.7 %all-to-all-done = bf16[2,8,256,1024]{2,1,0,3:T(8,128)(2,1)} async-done(((bf16[2,8,256,1024]{2,1,0,3:T(8,128)(2,1)}), bf16[2,8,256,1024]{2,1,0,3:T(8,128)(2,1)}, u32[]{:S(2)}, u32[]{:S(2)}) %all-to-all-start) | async-done | bytes 8388640 | tf_op jit(solution)/shard_map/all_to_all | solution.py:71
  209.6 5.0 all-to-all-start.1
  214.6 0.0 all-gather.2.cloned.1.call-start
  214.7 12.5 %copy.9 = bf16[2,8,256,8,128]{4,2,1,3,0:T(8,128)(2,1)} copy(bf16[2,8,256,8,128]{2,1,0,4,3:T(8,128)(2,1)} %bitcast.1) | data formatting | bytes 16777216 | tf_op jit(solution)/shard_map/all_to_all | solution.py:71
  227.2 5.3 slice_bitcast_fusion.8
  232.5 14.0 %fusion.28 = f32[64,32768]{1,0:T(8,128)} fusion(bf16[8,8,256,128]{3,2,1,0:T(8,128)(2,1)S(1)} %get-tuple-element.12, s32[64]{0:T(128)S(1)} %get-tuple-element.13, s32[64]{0:T(128)S(1)} %get-tuple-element.14, s32[64]{0:T(128)S(1)} %and_select_fusion.3), kind=kOutput, calls=%fused_computation.48 | convolution fusion | flops 1610690560 | bytes 12583680 | tf_op jit(solution)/shard_map/dot_general | solution.py:30
  246.5 14.5 %fusion.30 = f32[64,32768]{1,0:T(8,128)} fusion(bf16[8,8,256,128]{3,2,1,0:T(8,128)(2,1)S(1)} %get-tuple-element.12, s32[64]{0:T(128)S(1)} %get-tuple-element.13, s32[64]{0:T(128)S(1)} %get-tuple-element.14, s32[64]{0:T(128)S(1)} %and_select_fusion.3), kind=kOutput, calls=%fused_computation.50 | convolution fusion | flops 1610690560 | bytes 12583680 | tf_op jit(solution)/shard_map/dot_general | solution.py:28
  261.0 135.8 %all-to-all-done.1 = bf16[2,8,256,1024]{2,1,0,3:T(8,128)(2,1)} async-done(((bf16[2,8,256,1024]{2,1,0,3:T(8,128)(2,1)}), bf16[2,8,256,1024]{2,1,0,3:T(8,128)(2,1)}, u32[]{:S(2)}, u32[]{:S(2)}) %all-to-all-start.1) | async-done | bytes 8388640 | tf_op jit(solution)/shard_map/all_to_all | solution.py:72
  396.9 12.2 %copy.11 = bf16[2,8,256,8,128]{4,2,1,3,0:T(8,128)(2,1)} copy(bf16[2,8,256,8,128]{2,1,0,4,3:T(8,128)(2,1)} %bitcast.3) | data formatting | bytes 16777216 | tf_op jit(solution)/shard_map/all_to_all | solution.py:72
  409.1 4.0 slice_bitcast_fusion.6
  413.1 5.4 fusion.22
  418.4 5.4 fusion.24
  423.9 0.0 slice-start.2
  423.9 14.6 %convolution_add_fusion = f32[64,32768]{1,0:T(8,128)} fusion(f32[64,32768]{1,0:T(8,128)S(1)} %fusion.22, bf16[8,8,256,128]{3,2,1,0:T(8,128)(2,1)S(1)} %get-tuple-element.9, s32[64]{0:T(128)S(1)} %get-tuple-element.13, s32[64]{0:T(128)S(1)} %get-tuple-element.14, s32[64]{0:T(128)S(1)} %and_select_fusion.3), kind=kOutput, calls=%fused_computation | convolution fusion | flops 1612787712 | bytes 20972288 | tf_op jit(solution)/shard_map/dot_general | solution.py:31
  438.5 0.0 copy-start.1
  438.5 0.0 slice-start.3
  438.5 14.7 %convolution_subtract_fusion = f32[64,32768]{1,0:T(8,128)} fusion(f32[64,32768]{1,0:T(8,128)S(1)} %fusion.24, bf16[8,8,256,128]{3,2,1,0:T(8,128)(2,1)S(1)} %get-tuple-element.9, s32[64]{0:T(128)S(1)} %get-tuple-element.13, s32[64]{0:T(128)S(1)} %get-tuple-element.14, s32[64]{0:T(128)S(1)} %and_select_fusion.3), kind=kOutput, calls=%fused_computation.2 | convolution fusion | flops 1612787712 | bytes 20972288 | tf_op jit(solution)/shard_map/dot_general | solution.py:29
  453.2 0.0 slice-done.2
  453.2 0.0 copy-done.1
  453.3 0.0 slice-done.3
  453.3 14.4 %convolution_subtract_fusion.1 = f32[64,32768]{1,0:T(8,128)} fusion(f32[64,32768]{1,0:T(8,128)S(1)} %bitcast.119, bf16[8,8,256,128]{3,2,1,0:T(8,128)(2,1)S(1)} %copy-done.1, s32[64]{0:T(128)S(1)} %get-tuple-element.13, s32[64]{0:T(128)S(1)} %get-tuple-element.14, s32[64]{0:T(128)S(1)} %and_select_fusion.3), kind=kOutput, calls=%fused_computation.3 | convolution fusion | flops 1612787712 | bytes 20972288 | tf_op jit(solution)/shard_map/dot_general | solution.py:29
  467.7 22.5 %multiply_subtract_fusion = (f32[64,32768]{1,0:T(8,128)}, f32[64,32768]{1,0:T(8,128)}) fusion(f32[64,32768]{1,0:T(8,128)} %convolution_add_fusion, f32[64,32768]{1,0:T(8,128)} %convolution_subtract_fusion.1, f32[64,32768]{1,0:T(8,128)} %convolution_subtract_fusion, f32[64,32768]{1,0:T(8,128)} %fusion.28, bf16[8,8,256,128]{3,2,1,0:T(8,128)(2,1)} %get-tuple-element.11, ...), kind=kOutput, calls=%fused_computation.35 | convolution fusion | flops 1625370624 | bytes 54526720 | tf_op jit(solution)/shard_map/dot_general | solution.py:31
  490.2 0.0 copy-start
  490.2 12.3 %fusion.50 = f32[64,32768]{1,0:T(8,128)} fusion(f32[64,32768]{1,0:T(8,128)} %get-tuple-element.5, s32[64]{0:T(128)S(1)} %get-tuple-element.13, s32[64]{0:T(128)S(1)} %get-tuple-element.14, s32[64]{0:T(128)S(1)} %and_select_fusion.3), kind=kOutput, calls=%fused_computation.77 | convolution fusion | flops 1610690560 | bytes 16777984 | tf_op jit(solution)/shard_map/dot_general | solution.py:37
  502.5 0.0 copy-done
  502.5 0.0 slice-start
  502.6 7.8 fusion.49
  510.3 0.0 slice-start.1
  510.3 12.9 %fusion.45 = bf16[8,8,256,128]{3,1,2,0:T(8,128)(2,1)} fusion(f32[64,32768]{1,0:T(8,128)} %fusion.50, f32[64,32768]{1,0:T(8,128)S(1)} %copy-done, s32[64]{0:T(128)S(1)} %get-tuple-element.13, s32[64]{0:T(128)S(1)} %get-tuple-element.14, s32[64]{0:T(128)S(1)} %and_select_fusion.3), kind=kOutput, calls=%fused_computation.67 | convolution fusion | flops 1614884864 | bytes 20972288 | tf_op jit(solution)/shard_map/dot_general | solution.py:38
  523.3 0.0 slice-done
  523.3 0.0 slice-done.1
  523.3 8.9 fusion.44
  532.1 0.0 copy-start.2
  532.2 1.2 copy.20
  533.3 0.5 bitcast_bitcast_fusion
  533.8 0.5 copy-done.2
  534.3 1.2 copy.19
  535.5 2.2 bitcast_bitcast_fusion.1
  537.7 6.4 pad_maximum_fusion
  544.1 187.9 %all_to_all.45 = bf16[2,64,256,128]{3,2,0,1:T(8,128)(2,1)} all-to-all(bf16[2,64,256,128]{3,2,0,1:T(8,128)(2,1)} %pad_maximum_fusion), channel_id=1, replica_groups=mesh['kt'=8,'tile'=4] {'kt'}, dimensions={1} | all-to-all | bytes 16777216 | tf_op jit(solution)/shard_map/all_to_all | solution.py:81
  732.0 13.9 %copy.56 = bf16[2,8,8,256,128]{4,1,3,2,0:T(8,128)(2,1)} copy(bf16[2,8,8,256,128]{4,3,0,2,1:T(8,128)(2,1)} %bitcast.123) | data formatting | bytes 16777216 | tf_op jit(solution)/shard_map/all_to_all | solution.py:81
  745.9 5.8 fusion.116
  751.6 7.3 squeeze.43
  759.0 7.4 squeeze.41
  766.4 0.0 copy-start.3
  766.4 15.1 %fusion.2 = f32[8,256,1024]{2,1,0:T(8,128)} fusion(bf16[8,256,1024]{2,1,0:T(8,128)(2,1)} %squeeze.41, bf16[2,8,1024,1024]{3,2,1,0:T(8,128)(2,1)} %param.5), kind=kOutput, calls=%fused_computation.11 | convolution fusion | flops 4294967296 | bytes 29360128 | tf_op jit(solution)/shard_map/kij,kjl->kil/dot_general | solution.py:59
  781.5 0.0 copy-done.3
  781.5 13.6 %fusion.4 = f32[8,256,1024]{2,1,0:T(8,128)} fusion(bf16[8,256,1024]{2,1,0:T(8,128)(2,1)S(1)} %copy-done.3, bf16[2,8,1024,1024]{3,2,1,0:T(8,128)(2,1)} %param.5), kind=kOutput, calls=%fused_computation.13 | convolution fusion | flops 4294967296 | bytes 29360128 | tf_op jit(solution)/shard_map/kij,kjl->kil/dot_general | solution.py:59
  795.1 14.8 %fusion.19 = bf16[1,8,256,1024]{3,2,1,0:T(8,128)(2,1)} fusion(f32[8,256,1024]{2,1,0:T(8,128)} %fusion.2, bf16[8,256,1024]{2,1,0:T(8,128)(2,1)S(1)} %copy-done.3, bf16[2,8,1024,1024]{3,2,1,0:T(8,128)(2,1)} %param.5), kind=kOutput, calls=%fused_computation.37 | convolution fusion | flops 4299161600 | bytes 33554432 | tf_op jit(solution)/shard_map/kij,kjl->kil/dot_general | solution.py:59
  809.9 0.0 copy-start.4
  809.9 13.7 %fusion.18 = bf16[1,8,256,1024]{3,2,1,0:T(8,128)(2,1)} fusion(f32[8,256,1024]{2,1,0:T(8,128)} %fusion.4, bf16[8,256,1024]{2,1,0:T(8,128)(2,1)} %squeeze.41, bf16[2,8,1024,1024]{3,2,1,0:T(8,128)(2,1)} %param.5), kind=kOutput, calls=%fused_computation.36 | convolution fusion | flops 4299161600 | bytes 33554432 | tf_op jit(solution)/shard_map/kij,kjl->kil/dot_general | solution.py:59
  823.6 0.0 copy-done.4
  823.6 6.4 pad_maximum_fusion.1
  830.0 0.0 all-gather.2.cloned.1.call-update
  830.0 200.5 %all-gather.2.cloned.1.call-done = bf16[2,8,1024,1024]{3,2,1,0:T(8,128)(2,1)} async-done(((bf16[2,8,256,1024]{3,2,1,0:T(8,128)(2,1)}), bf16[2,8,1024,1024]{3,2,1,0:T(8,128)(2,1)}) %all-gather.2.cloned.1.call-update) | async-done | bytes 33554448 | tf_op jit(solution)/shard_map/all_gather | solution.py:86
  1030.5 14.8 %fusion.11 = f32[8,256,1024]{2,1,0:T(8,128)} fusion(bf16[2,8,1024,1024]{3,2,1,0:T(8,128)(2,1)} %all-gather.2.cloned.1.call-done, bf16[2,8,1024,1024]{3,2,1,0:T(8,128)(2,1)} %param.5, s32[]{:T(128)S(6)} %select_n.170), kind=kOutput, calls=%fused_computation.20 | convolution fusion | flops 4294967296 | bytes 29360132 | tf_op jit(solution)/shard_map/kij,kjl->kil/dot_general | solution.py:59
  1045.3 15.0 %fusion.10 = f32[8,256,1024]{2,1,0:T(8,128)} fusion(bf16[2,8,1024,1024]{3,2,1,0:T(8,128)(2,1)} %all-gather.2.cloned.1.call-done, bf16[2,8,1024,1024]{3,2,1,0:T(8,128)(2,1)} %param.5, s32[]{:T(128)S(6)} %add.203, s32[]{:T(128)S(6)} %select_n.170), kind=kOutput, calls=%fused_computation.19 | convolution fusion | flops 4294967296 | bytes 29360136 | tf_op jit(solution)/shard_map/kij,kjl->kil/dot_general | solution.py:59
  1060.3 17.2 %add_bitcast_fusion = f32[1,8,256,1024]{3,2,1,0:T(8,128)} fusion(f32[8,256,1024]{2,1,0:T(8,128)} %fusion.10, bf16[2,8,1024,1024]{3,2,1,0:T(8,128)(2,1)} %all-gather.2.cloned.1.call-done, bf16[2,8,1024,1024]{3,2,1,0:T(8,128)(2,1)} %param.5, s32[]{:T(128)S(6)} %select_n.170), kind=kOutput, calls=%fused_computation.30 | convolution fusion | flops 4297064448 | bytes 37748740 | tf_op jit(solution)/shard_map/kij,kjl->kil/dot_general | solution.py:59
  1077.5 17.5 %subtract_bitcast_fusion = f32[1,8,256,1024]{3,2,1,0:T(8,128)} fusion(f32[8,256,1024]{2,1,0:T(8,128)} %fusion.11, bf16[2,8,1024,1024]{3,2,1,0:T(8,128)(2,1)} %all-gather.2.cloned.1.call-done, bf16[2,8,1024,1024]{3,2,1,0:T(8,128)(2,1)} %param.5, s32[]{:T(128)S(6)} %add.203, s32[]{:T(128)S(6)} %select_n.170), kind=kOutput, calls=%fused_computation.31 | convolution fusion | flops 4297064448 | bytes 37748744 | tf_op jit(solution)/shard_map/kij,kjl->kil/dot_general | solution.py:59
  1095.0 14.7 %maximum_add_fusion = f32[2,8,256,1024]{3,2,1,0:T(8,128)} fusion(f32[1,8,256,1024]{3,2,1,0:T(8,128)} %add_bitcast_fusion, f32[1,8,256,1024]{3,2,1,0:T(8,128)} %subtract_bitcast_fusion, bf16[2,8,1024,1024]{3,2,1,0:T(8,128)(2,1)} %param.5, s32[]{:T(128)S(6)} %select_n.170), kind=kLoop, calls=%fused_computation.10 | loop fusion | flops 12582912 | bytes 41943044 | tf_op jit(solution)/shard_map/add | solution.py:91
  (4 shorter events, 0.0 us)
Async XLA Ops:
  19.1 190.5 %all-to-all-start = ((bf16[2,8,256,1024]{2,1,0,3:T(8,128)(2,1)}), bf16[2,8,256,1024]{2,1,0,3:T(8,128)(2,1)}, u32[]{:S(2)}, u32[]{:S(2)}) async-start(bf16[2,8,256,1024]{2,1,0,3:T(8,128)(2,1)} %copy.8), calls=%async_computation | async-start | bytes 16777216 | tf_op jit(solution)/shard_map/all_to_all | solution.py:71
  209.6 187.3 %all-to-all-start.1 = ((bf16[2,8,256,1024]{2,1,0,3:T(8,128)(2,1)}), bf16[2,8,256,1024]{2,1,0,3:T(8,128)(2,1)}, u32[]{:S(2)}, u32[]{:S(2)}) async-start(bf16[2,8,256,1024]{2,1,0,3:T(8,128)(2,1)} %copy.10), calls=%async_computation.1 | async-start | bytes 16777216 | tf_op jit(solution)/shard_map/all_to_all | solution.py:72
  214.6 815.9 %all-gather.2.cloned.1.call-start = ((), (), s32[]{:S(2)}) async-start(), calls=%async_computation.3 | async-start | bytes 41943040 | tf_op jit(solution)/shard_map/all_gather | solution.py:86
  423.9 29.4 %slice-start.2 = ((s8[8388608]{0:T(1024)(128)(4,1)}), s8[4194304]{0:T(1024)(128)(4,1)S(1)}, s32[]{:S(2)}) async-start(s8[8388608]{0:T(1024)(128)(4,1)} %bitcast.118), calls=%async_computation.6 | async-start | bytes 8388608
  438.5 14.8 %copy-start.1 = (bf16[8,8,256,128]{3,2,1,0:T(8,128)(2,1)S(1)}, bf16[8,8,256,128]{3,2,1,0:T(8,128)(2,1)}, u32[]{:S(2)}) copy-start(bf16[8,8,256,128]{3,2,1,0:T(8,128)(2,1)} %get-tuple-element.11) | copy-start | bytes 12582916
  438.5 14.8 %slice-start.3 = ((s8[8388608]{0:T(1024)(128)(4,1)}), s8[4194304]{0:T(1024)(128)(4,1)S(1)}, s32[]{:S(2)}) async-start(s8[8388608]{0:T(1024)(128)(4,1)} %bitcast.118), calls=%async_computation.7 | async-start | bytes 8388608
  490.2 12.3 %copy-start = (f32[64,32768]{1,0:T(8,128)S(1)}, f32[64,32768]{1,0:T(8,128)}, u32[]{:S(2)}) copy-start(f32[64,32768]{1,0:T(8,128)} %get-tuple-element.6) | copy-start | bytes 25165828
  502.5 20.7 %slice-start = ((s8[8388608]{0:T(1024)(128)(4,1)}), s8[4194304]{0:T(1024)(128)(4,1)S(1)}, s32[]{:S(2)}) async-start(s8[8388608]{0:T(1024)(128)(4,1)} %bitcast.116), calls=%async_computation.4 | async-start | bytes 8388608
  510.3 12.9 %slice-start.1 = ((s8[8388608]{0:T(1024)(128)(4,1)}), s8[4194304]{0:T(1024)(128)(4,1)S(1)}, s32[]{:S(2)}) async-start(s8[8388608]{0:T(1024)(128)(4,1)} %bitcast.116), calls=%async_computation.5 | async-start | bytes 8388608
  532.1 2.2 copy-start.2
  766.4 15.1 %copy-start.3 = (bf16[8,256,1024]{2,1,0:T(8,128)(2,1)S(1)}, bf16[8,256,1024]{2,1,0:T(8,128)(2,1)}, u32[]{:S(2)}) copy-start(bf16[8,256,1024]{2,1,0:T(8,128)(2,1)} %squeeze.43) | copy-start | bytes 12582916
  809.9 13.8 %copy-start.4 = (bf16[1,8,256,1024]{3,2,1,0:T(8,128)(2,1)S(1)}, bf16[1,8,256,1024]{3,2,1,0:T(8,128)(2,1)}, u32[]{:S(2)}) copy-start(bf16[1,8,256,1024]{3,2,1,0:T(8,128)(2,1)} %fusion.19) | copy-start | bytes 12582916
Sparse Core Ops, SparseCore 0:
  830.1 200.3 all-gather.1
where the time goes:
time: 1120 us
  waiting for transfers between devices  507 us (45%)
  matrix products  269 us (24%)
  blocking collectives  188 us (17%)
  local copies, waits for them, and re-layouts  99 us (9%)
  other arithmetic  27.4 us (2%)
  between operations  14 us (1%)
  starting transfers between devices  12.4 us (1%)
    all_gather x1, waiting for transfers between devices, body(): segment = lax.all_gather(mid_stack, 'tile', axis=2, tiled=True)  201 us
    all_to_all x1, blocking collectives, body(): lax.all_to_all(polar_q, 'kt', split_axis=1, concat_axis=3, tiled=True)  188 us
    all_to_all x1, waiting for transfers between devices, body(): lax.all_to_all(green_particle, 'kt', split_axis=3, concat_axis=1, tiled=T...  171 us
    all_to_all x1, waiting for transfers between devices, body(): lax.all_to_all(green_hole, 'kt', split_axis=3, concat_axis=1, tiled=True)  136 us
    dot_general x8, matrix products, product_of(): jnp.einsum('kij,kjl->kil', left_side, right_side, preferred_element_type=...  122 us
    unnamed x24, local copies, waits for them, and re-layouts  37.2 us
    dot_general x2, matrix products, to_cells(): jnp.dot(cosine_table, imag_part, precision=HIGHEST)  37.1 us
    dot_general x2, matrix products, to_cells(): jnp.dot(sine_table, imag_part, precision=HIGHEST)  29.1 us
  transfers between devices with their start and end apart: 3, of which 3 were waited for; matrix products, arithmetic and copies ran while one was open for 5% of the time, Pallas kernels for 0%

commit v1 on v0

--- a/solution.py
+++ b/solution.py
@@ -78,7 +78,10 @@
         moved_hole.reshape(2, points, tile_rows * narrow),
     )
     polar_q = polar_q.reshape(2, points, tile_rows, narrow)
-    polar_rows = lax.all_to_all(polar_q, "kt", split_axis=1, concat_axis=3, tiled=True)
+    polar_rows = jnp.concatenate(
+        lax.all_to_all(jnp.stack(jnp.split(polar_q, lax.axis_size("kt"), axis=1)), "kt", 0, 0),
+        axis=3,
+    )
     mid_real, mid_imag = complex_batched(polar_rows[0], polar_rows[1], coulomb[0], coulomb[1])
     mid_stack = jnp.stack([mid_real.astype(jnp.bfloat16), mid_imag.astype(jnp.bfloat16)])
     row_start = lax.axis_index("tile") * tile_rows

time: 1120 us -> 1120 us (level)
    all_to_all x1 -> x0, local copies, waits for them, and re-layouts: 13.9 us -> none  [body(): lax.all_to_all(polar_q, 'kt', split_axis=1, concat_axis=3, tiled=True)]
    unnamed x24 -> x32, local copies, waits for them, and re-layouts: 37.2 us -> 40.4 us
where the time goes in v1:
time: 1120 us; the launch traced here: 1110 us
  waiting for transfers between devices  507 us (45%)
  matrix products  271 us (24%)
  blocking collectives  187 us (17%)
  local copies, waits for them, and re-layouts  94.8 us (8%)
  other arithmetic  21 us (2%)
  between operations  14.1 us (1%)
  starting transfers between devices  12.4 us (1%)
    all_gather x1, waiting for transfers between devices, body(): segment = lax.all_gather(mid_stack, 'tile', axis=2, tiled=True)  201 us
    all_to_all x1, blocking collectives, body(): lax.all_to_all(jnp.stack(jnp.split(polar_q, lax.axis_size('kt'), axis=1))...  187 us
    all_to_all x1, waiting for transfers between devices, body(): lax.all_to_all(green_particle, 'kt', split_axis=3, concat_axis=1, tiled=T...  171 us
    all_to_all x1, waiting for transfers between devices, body(): lax.all_to_all(green_hole, 'kt', split_axis=3, concat_axis=1, tiled=True)  136 us
    dot_general x8, matrix products, product_of(): jnp.einsum('kij,kjl->kil', left_side, right_side, preferred_element_type=...  122 us
    unnamed x32, local copies, waits for them, and re-layouts  40.4 us
    dot_general x2, matrix products, to_cells(): jnp.dot(cosine_table, imag_part, precision=HIGHEST)  37.1 us
    dot_general x2, matrix products, to_cells(): jnp.dot(sine_table, imag_part, precision=HIGHEST)  29.2 us
  transfers between devices with their start and end apart: 3, of which 3 were waited for; matrix products, arithmetic and copies ran while one was open for 5% of the time, Pallas kernels for 0%

profile of v1, /device:TPU:0, one launch (start us, length us, event | category | flops | bytes accessed | tf_op | source)
XLA Modules:
  0.0 1107.2 jit_solution(12600023614240701714)
XLA Ops:
  6.5 12.6 %copy.10 = bf16[2,8,256,1024]{2,1,0,3:T(8,128)(2,1)} copy(bf16[2,8,256,1024]{3,2,1,0:T(8,128)(2,1)} %param.3) | data formatting | bytes 16777216 | tf_op args[0]
  19.1 7.3 all-to-all-start
  26.4 12.5 %copy.12 = bf16[2,8,256,1024]{2,1,0,3:T(8,128)(2,1)} copy(bf16[2,8,256,1024]{3,2,1,0:T(8,128)(2,1)} %param.4) | data formatting | bytes 16777216 | tf_op args[1]
  38.9 170.7 %all-to-all-done = bf16[2,8,256,1024]{2,1,0,3:T(8,128)(2,1)} async-done(((bf16[2,8,256,1024]{2,1,0,3:T(8,128)(2,1)}), bf16[2,8,256,1024]{2,1,0,3:T(8,128)(2,1)}, u32[]{:S(2)}, u32[]{:S(2)}) %all-to-all-start) | async-done | bytes 8388640 | tf_op jit(solution)/shard_map/all_to_all | solution.py:71
  209.6 5.0 all-to-all-start.1
  214.6 0.0 all-gather.2.cloned.1.call-start
  214.7 12.5 %copy.11 = bf16[2,8,256,8,128]{4,2,1,3,0:T(8,128)(2,1)} copy(bf16[2,8,256,8,128]{2,1,0,4,3:T(8,128)(2,1)} %bitcast.1) | data formatting | bytes 16777216 | tf_op jit(solution)/shard_map/all_to_all | solution.py:71
  227.2 5.3 slice_bitcast_fusion.8
  232.5 14.0 %fusion.28 = f32[64,32768]{1,0:T(8,128)} fusion(bf16[8,8,256,128]{3,2,1,0:T(8,128)(2,1)S(1)} %get-tuple-element.12, s32[64]{0:T(128)S(1)} %get-tuple-element.13, s32[64]{0:T(128)S(1)} %get-tuple-element.14, s32[64]{0:T(128)S(1)} %and_select_fusion.3), kind=kOutput, calls=%fused_computation.46 | convolution fusion | flops 1610690560 | bytes 12583680 | tf_op jit(solution)/shard_map/dot_general | solution.py:30
  246.5 14.5 %fusion.30 = f32[64,32768]{1,0:T(8,128)} fusion(bf16[8,8,256,128]{3,2,1,0:T(8,128)(2,1)S(1)} %get-tuple-element.12, s32[64]{0:T(128)S(1)} %get-tuple-element.13, s32[64]{0:T(128)S(1)} %get-tuple-element.14, s32[64]{0:T(128)S(1)} %and_select_fusion.3), kind=kOutput, calls=%fused_computation.48 | convolution fusion | flops 1610690560 | bytes 12583680 | tf_op jit(solution)/shard_map/dot_general | solution.py:28
  261.0 135.8 %all-to-all-done.1 = bf16[2,8,256,1024]{2,1,0,3:T(8,128)(2,1)} async-done(((bf16[2,8,256,1024]{2,1,0,3:T(8,128)(2,1)}), bf16[2,8,256,1024]{2,1,0,3:T(8,128)(2,1)}, u32[]{:S(2)}, u32[]{:S(2)}) %all-to-all-start.1) | async-done | bytes 8388640 | tf_op jit(solution)/shard_map/all_to_all | solution.py:72
  396.9 12.2 %copy.13 = bf16[2,8,256,8,128]{4,2,1,3,0:T(8,128)(2,1)} copy(bf16[2,8,256,8,128]{2,1,0,4,3:T(8,128)(2,1)} %bitcast.3) | data formatting | bytes 16777216 | tf_op jit(solution)/shard_map/all_to_all | solution.py:72
  409.1 4.0 slice_bitcast_fusion.6
  413.1 5.4 fusion.22
  418.4 5.4 fusion.24
  423.9 0.0 slice-start.2
  423.9 14.6 %convolution_add_fusion = f32[64,32768]{1,0:T(8,128)} fusion(f32[64,32768]{1,0:T(8,128)S(1)} %fusion.22, bf16[8,8,256,128]{3,2,1,0:T(8,128)(2,1)S(1)} %get-tuple-element.9, s32[64]{0:T(128)S(1)} %get-tuple-element.13, s32[64]{0:T(128)S(1)} %get-tuple-element.14, s32[64]{0:T(128)S(1)} %and_select_fusion.3), kind=kOutput, calls=%fused_computation | convolution fusion | flops 1612787712 | bytes 20972288 | tf_op jit(solution)/shard_map/dot_general | solution.py:31
  438.4 14.8 %convolution_subtract_fusion = f32[64,32768]{1,0:T(8,128)} fusion(f32[64,32768]{1,0:T(8,128)S(1)} %fusion.24, bf16[8,8,256,128]{3,2,1,0:T(8,128)(2,1)S(1)} %get-tuple-element.9, s32[64]{0:T(128)S(1)} %get-tuple-element.13, s32[64]{0:T(128)S(1)} %get-tuple-element.14, s32[64]{0:T(128)S(1)} %and_select_fusion.3), kind=kOutput, calls=%fused_computation.2 | convolution fusion | flops 1612787712 | bytes 20972288 | tf_op jit(solution)/shard_map/dot_general | solution.py:29
  453.2 0.0 slice-done.2
  453.2 0.0 copy-done.1
  453.3 0.0 slice-done.3
  453.3 14.4 %convolution_subtract_fusion.1 = f32[64,32768]{1,0:T(8,128)} fusion(f32[64,32768]{1,0:T(8,128)S(1)} %bitcast.144, bf16[8,8,256,128]{3,2,1,0:T(8,128)(2,1)S(1)} %copy-done.1, s32[64]{0:T(128)S(1)} %get-tuple-element.13, s32[64]{0:T(128)S(1)} %get-tuple-element.14, s32[64]{0:T(128)S(1)} %and_select_fusion.3), kind=kOutput, calls=%fused_computation.3 | convolution fusion | flops 1612787712 | bytes 20972288 | tf_op jit(solution)/shard_map/dot_general | solution.py:29
  467.7 22.5 %multiply_add_fusion = (f32[64,32768]{1,0:T(8,128)}, f32[64,32768]{1,0:T(8,128)}) fusion(f32[64,32768]{1,0:T(8,128)} %convolution_subtract_fusion, f32[64,32768]{1,0:T(8,128)} %convolution_subtract_fusion.1, f32[64,32768]{1,0:T(8,128)} %convolution_add_fusion, f32[64,32768]{1,0:T(8,128)} %fusion.28, bf16[8,8,256,128]{3,2,1,0:T(8,128)(2,1)} %get-tuple-element.11, ...), kind=kOutput, calls=%fused_computation.32 | convolution fusion | flops 1625370624 | bytes 54526720 | tf_op jit(solution)/shard_map/dot_general | solution.py:31
  490.2 12.3 %fusion.57 = f32[64,32768]{1,0:T(8,128)} fusion(f32[64,32768]{1,0:T(8,128)} %get-tuple-element.5, s32[64]{0:T(128)S(1)} %get-tuple-element.13, s32[64]{0:T(128)S(1)} %get-tuple-element.14, s32[64]{0:T(128)S(1)} %and_select_fusion.3), kind=kOutput, calls=%fused_computation.90 | convolution fusion | flops 1610690560 | bytes 16777984 | tf_op jit(solution)/shard_map/dot_general | solution.py:39
  502.5 0.0 copy-done
  502.6 7.8 fusion.58
  510.3 0.0 slice-start.1
  510.3 12.9 %fusion.44 = bf16[8,8,256,128]{3,1,2,0:T(8,128)(2,1)} fusion(f32[64,32768]{1,0:T(8,128)} %fusion.57, f32[64,32768]{1,0:T(8,128)S(1)} %copy-done, s32[64]{0:T(128)S(1)} %get-tuple-element.13, s32[64]{0:T(128)S(1)} %get-tuple-element.14, s32[64]{0:T(128)S(1)} %and_select_fusion.3), kind=kOutput, calls=%fused_computation.64 | convolution fusion | flops 1614884864 | bytes 20972288 | tf_op jit(solution)/shard_map/dot_general | solution.py:40
  523.3 0.0 slice-done
  523.3 0.0 slice-done.1
  523.3 10.8 fusion.45
  534.1 0.0 copy-start.2
  534.1 3.5 copy.20
  537.6 1.2 copy.21
  538.8 0.5 bitcast_dynamic-update-slice_fusion.1
  539.3 0.5 bitcast_dynamic-update-slice_fusion
  539.8 0.1 fusion.53
  539.9 0.1 fusion.52
  540.0 0.1 fusion.51
  540.2 0.1 fusion.50
  540.3 0.1 fusion.49
  540.5 0.1 fusion.48
  540.6 0.1 fusion.47
  540.8 0.1 fusion.46
  540.9 186.6 %all_to_all.35 = bf16[8,2,8,256,128]{4,3,2,1,0:T(8,128)(2,1)S(1)} all-to-all(bf16[8,2,8,256,128]{4,3,2,1,0:T(8,128)(2,1)S(1)} %fusion.46), channel_id=1, replica_groups=mesh['kt'=8,'tile'=4] {'kt'}, dimensions={0} | all-to-all | bytes 16777216 | tf_op jit(solution)/shard_map/all_to_all | solution.py:82
  727.5 2.5 fusion.124
  730.0 4.8 copy.15
  734.9 7.3 squeeze.43
  742.1 6.9 copy.14
  749.0 7.4 squeeze.41
  756.5 15.1 %fusion.2 = f32[8,256,1024]{2,1,0:T(8,128)} fusion(bf16[8,256,1024]{2,1,0:T(8,128)(2,1)} %squeeze.41, bf16[2,8,1024,1024]{3,2,1,0:T(8,128)(2,1)} %param.5), kind=kOutput, calls=%fused_computation.11 | convolution fusion | flops 4294967296 | bytes 29360128 | tf_op jit(solution)/shard_map/kij,kjl->kil/dot_general | solution.py:59
  771.6 0.0 copy-done.3
  771.6 13.6 %fusion.4 = f32[8,256,1024]{2,1,0:T(8,128)} fusion(bf16[8,256,1024]{2,1,0:T(8,128)(2,1)S(1)} %copy-done.3, bf16[2,8,1024,1024]{3,2,1,0:T(8,128)(2,1)} %param.5), kind=kOutput, calls=%fused_computation.13 | convolution fusion | flops 4294967296 | bytes 29360128 | tf_op jit(solution)/shard_map/kij,kjl->kil/dot_general | solution.py:59
  785.2 14.7 %fusion.19 = bf16[1,8,256,1024]{3,2,1,0:T(8,128)(2,1)} fusion(f32[8,256,1024]{2,1,0:T(8,128)} %fusion.2, bf16[8,256,1024]{2,1,0:T(8,128)(2,1)S(1)} %copy-done.3, bf16[2,8,1024,1024]{3,2,1,0:T(8,128)(2,1)} %param.5), kind=kOutput, calls=%fused_computation.35 | convolution fusion | flops 4299161600 | bytes 33554432 | tf_op jit(solution)/shard_map/kij,kjl->kil/dot_general | solution.py:59
  799.9 13.7 %fusion.18 = bf16[1,8,256,1024]{3,2,1,0:T(8,128)(2,1)} fusion(f32[8,256,1024]{2,1,0:T(8,128)} %fusion.4, bf16[8,256,1024]{2,1,0:T(8,128)(2,1)} %squeeze.41, bf16[2,8,1024,1024]{3,2,1,0:T(8,128)(2,1)} %param.5), kind=kOutput, calls=%fused_computation.34 | convolution fusion | flops 4299161600 | bytes 33554432 | tf_op jit(solution)/shard_map/kij,kjl->kil/dot_general | solution.py:59
  813.7 0.0 copy-done.4
  813.7 6.4 pad_maximum_fusion
  820.0 0.0 all-gather.2.cloned.1.call-update
  820.1 200.7 %all-gather.2.cloned.1.call-done = bf16[2,8,1024,1024]{3,2,1,0:T(8,128)(2,1)} async-done(((bf16[2,8,256,1024]{3,2,1,0:T(8,128)(2,1)}), bf16[2,8,1024,1024]{3,2,1,0:T(8,128)(2,1)}) %all-gather.2.cloned.1.call-update) | async-done | bytes 33554448 | tf_op jit(solution)/shard_map/all_gather | solution.py:89
  1020.8 14.8 %fusion.11 = f32[8,256,1024]{2,1,0:T(8,128)} fusion(bf16[2,8,1024,1024]{3,2,1,0:T(8,128)(2,1)} %all-gather.2.cloned.1.call-done, bf16[2,8,1024,1024]{3,2,1,0:T(8,128)(2,1)} %param.5, s32[]{:T(128)S(6)} %select_n.170), kind=kOutput, calls=%fused_computation.20 | convolution fusion | flops 4294967296 | bytes 29360132 | tf_op jit(solution)/shard_map/kij,kjl->kil/dot_general | solution.py:59
  1035.6 15.0 %fusion.10 = f32[8,256,1024]{2,1,0:T(8,128)} fusion(bf16[2,8,1024,1024]{3,2,1,0:T(8,128)(2,1)} %all-gather.2.cloned.1.call-done, bf16[2,8,1024,1024]{3,2,1,0:T(8,128)(2,1)} %param.5, s32[]{:T(128)S(6)} %add.203, s32[]{:T(128)S(6)} %select_n.170), kind=kOutput, calls=%fused_computation.19 | convolution fusion | flops 4294967296 | bytes 29360136 | tf_op jit(solution)/shard_map/kij,kjl->kil/dot_general | solution.py:59
  1050.5 17.2 %add_bitcast_fusion = f32[1,8,256,1024]{3,2,1,0:T(8,128)} fusion(f32[8,256,1024]{2,1,0:T(8,128)} %fusion.10, bf16[2,8,1024,1024]{3,2,1,0:T(8,128)(2,1)} %all-gather.2.cloned.1.call-done, bf16[2,8,1024,1024]{3,2,1,0:T(8,128)(2,1)} %param.5, s32[]{:T(128)S(6)} %select_n.170), kind=kOutput, calls=%fused_computation.28 | convolution fusion | flops 4297064448 | bytes 37748740 | tf_op jit(solution)/shard_map/kij,kjl->kil/dot_general | solution.py:59
  1067.8 17.5 %subtract_bitcast_fusion = f32[1,8,256,1024]{3,2,1,0:T(8,128)} fusion(f32[8,256,1024]{2,1,0:T(8,128)} %fusion.11, bf16[2,8,1024,1024]{3,2,1,0:T(8,128)(2,1)} %all-gather.2.cloned.1.call-done, bf16[2,8,1024,1024]{3,2,1,0:T(8,128)(2,1)} %param.5, s32[]{:T(128)S(6)} %add.203, s32[]{:T(128)S(6)} %select_n.170), kind=kOutput, calls=%fused_computation.29 | convolution fusion | flops 4297064448 | bytes 37748744 | tf_op jit(solution)/shard_map/kij,kjl->kil/dot_general | solution.py:59
  1085.2 14.7 %maximum_add_fusion = f32[2,8,256,1024]{3,2,1,0:T(8,128)} fusion(f32[1,8,256,1024]{3,2,1,0:T(8,128)} %add_bitcast_fusion, f32[1,8,256,1024]{3,2,1,0:T(8,128)} %subtract_bitcast_fusion, bf16[2,8,1024,1024]{3,2,1,0:T(8,128)(2,1)} %param.5, s32[]{:T(128)S(6)} %select_n.170), kind=kLoop, calls=%fused_computation.10 | loop fusion | flops 12582912 | bytes 41943044 | tf_op jit(solution)/shard_map/add | solution.py:94
  (11 shorter events, 0.0 us)
Async XLA Ops:
  19.1 190.5 %all-to-all-start = ((bf16[2,8,256,1024]{2,1,0,3:T(8,128)(2,1)}), bf16[2,8,256,1024]{2,1,0,3:T(8,128)(2,1)}, u32[]{:S(2)}, u32[]{:S(2)}) async-start(bf16[2,8,256,1024]{2,1,0,3:T(8,128)(2,1)} %copy.10), calls=%async_computation | async-start | bytes 16777216 | tf_op jit(solution)/shard_map/all_to_all | solution.py:71
  209.6 187.3 %all-to-all-start.1 = ((bf16[2,8,256,1024]{2,1,0,3:T(8,128)(2,1)}), bf16[2,8,256,1024]{2,1,0,3:T(8,128)(2,1)}, u32[]{:S(2)}, u32[]{:S(2)}) async-start(bf16[2,8,256,1024]{2,1,0,3:T(8,128)(2,1)} %copy.12), calls=%async_computation.1 | async-start | bytes 16777216 | tf_op jit(solution)/shard_map/all_to_all | solution.py:72
  214.6 806.2 %all-gather.2.cloned.1.call-start = ((), (), s32[]{:S(2)}) async-start(), calls=%async_computation.3 | async-start | bytes 41943040 | tf_op jit(solution)/shard_map/all_gather | solution.py:89
  423.9 29.4 %slice-start.2 = ((s8[8388608]{0:T(1024)(128)(4,1)}), s8[4194304]{0:T(1024)(128)(4,1)S(1)}, s32[]{:S(2)}) async-start(s8[8388608]{0:T(1024)(128)(4,1)} %bitcast.143), calls=%async_computation.6 | async-start | bytes 8388608
  438.4 14.8 %copy-start.1 = (bf16[8,8,256,128]{3,2,1,0:T(8,128)(2,1)S(1)}, bf16[8,8,256,128]{3,2,1,0:T(8,128)(2,1)}, u32[]{:S(2)}) copy-start(bf16[8,8,256,128]{3,2,1,0:T(8,128)(2,1)} %get-tuple-element.11) | copy-start | bytes 12582916
  438.4 14.8 %slice-start.3 = ((s8[8388608]{0:T(1024)(128)(4,1)}), s8[4194304]{0:T(1024)(128)(4,1)S(1)}, s32[]{:S(2)}) async-start(s8[8388608]{0:T(1024)(128)(4,1)} %bitcast.143), calls=%async_computation.7 | async-start | bytes 8388608
  490.2 12.3 %copy-start = (f32[64,32768]{1,0:T(8,128)S(1)}, f32[64,32768]{1,0:T(8,128)}, u32[]{:S(2)}) copy-start(f32[64,32768]{1,0:T(8,128)} %get-tuple-element.6) | copy-start | bytes 25165828
  502.5 20.7 %slice-start = ((s8[8388608]{0:T(1024)(128)(4,1)}), s8[4194304]{0:T(1024)(128)(4,1)S(1)}, s32[]{:S(2)}) async-start(s8[8388608]{0:T(1024)(128)(4,1)} %bitcast.141), calls=%async_computation.4 | async-start | bytes 8388608
  510.3 12.9 %slice-start.1 = ((s8[8388608]{0:T(1024)(128)(4,1)}), s8[4194304]{0:T(1024)(128)(4,1)S(1)}, s32[]{:S(2)}) async-start(s8[8388608]{0:T(1024)(128)(4,1)} %bitcast.141), calls=%async_computation.5 | async-start | bytes 8388608
  534.1 3.5 copy-start.2
  756.5 15.1 %copy-start.3 = (bf16[8,256,1024]{2,1,0:T(8,128)(2,1)S(1)}, bf16[8,256,1024]{2,1,0:T(8,128)(2,1)}, u32[]{:S(2)}) copy-start(bf16[8,256,1024]{2,1,0:T(8,128)(2,1)} %squeeze.43) | copy-start | bytes 12582916
  799.9 13.8 %copy-start.4 = (bf16[1,8,256,1024]{3,2,1,0:T(8,128)(2,1)S(1)}, bf16[1,8,256,1024]{3,2,1,0:T(8,128)(2,1)}, u32[]{:S(2)}) copy-start(bf16[1,8,256,1024]{3,2,1,0:T(8,128)(2,1)} %fusion.19) | copy-start | bytes 12582916
Sparse Core Ops, SparseCore 0:
  820.2 200.5 all-gather.1
